TPU v7x, 32 devices: a whole 2x2x4 slice. The times are simulated.
32 devices in a mesh: row: 4 (over y, x), col: 4 (over z), layer: 2 (over core).
Axes of the slice: x: 2, y: 2, z: 4, core: 2. Of those that a mesh axis runs over, the one named last changes fastest.
Arguments:
- hamiltonian: bfloat16 [4096, 4096], P('row', 'col'), as said below
- start_vectors: bfloat16 [256, 4096], P('row', ('col', 'layer')), may hold values from -6 to 6
- cut_low: float32 [1], replicated, may hold values from -1.6 to -1.2
- cut_high: float32 [1], replicated, may hold values from 2 to 2.4
Outputs:
- filtered: bfloat16 [256, 4096], P('row', ('col', 'layer'))
Inputs may be any that keep to these rules, and one draw needn't show every extreme that they name: hamiltonian is exactly symmetric.
All inputs are finite; a program needn't handle non-finite values.
Results may differ from a plain program's by a relative error of at most 0.009.
Values may be sent and summed in bfloat16 or wider, within the bound.
No kernel may reach another device: no remote copies, remote signals or barrier semaphores. Data moves between devices by JAX's collectives and lax.ppermute only.
A program may use at most 64 MiB of HBM per device.

v0:
```python
import jax
import jax.numpy as jnp
from jax import lax
from jax.sharding import PartitionSpec as P


def make_shifted(block, first_row, first_col, centre, half_width):
    row_count, col_count = block.shape
    row_ids = lax.broadcasted_iota(jnp.int32, (row_count, col_count), 0) + first_row
    col_ids = lax.broadcasted_iota(jnp.int32, (row_count, col_count), 1) + first_col
    diagonal_mask = (row_ids == col_ids).astype(jnp.float32)
    return ((block.astype(jnp.float32) - centre * diagonal_mask) / half_width).astype(jnp.bfloat16)


def recurrence(begin, by_columns, by_rows):
    first = by_columns(begin).astype(jnp.bfloat16)
    second = (2.0 * by_rows(first) - begin.astype(jnp.float32)).astype(jnp.bfloat16)
    third = (2.0 * by_columns(second) - first.astype(jnp.float32)).astype(jnp.bfloat16)
    return (2.0 * by_rows(third) - second.astype(jnp.float32)).astype(jnp.bfloat16)


def local(hamiltonian, start_vectors, cut_low, cut_high):
    centre = (cut_low[0] + cut_high[0]) * 0.5
    half_width = (cut_high[0] - cut_low[0]) * 0.5
    row_count = hamiltonian.shape[0]
    first_row = lax.axis_index("row") * row_count
    width = hamiltonian.shape[1]
    whole = make_shifted(hamiltonian, first_row, lax.axis_index("col") * width, centre, half_width)

    def left_whole(panel):
        return lax.dot_general(
            panel, whole, (((1,), (1,)), ((), ())), preferred_element_type=jnp.float32
        )

    def right_whole(panel):
        return jnp.dot(panel, whole, preferred_element_type=jnp.float32)

    def by_columns(vectors):
        partial_value = left_whole(lax.all_gather(vectors, "row", axis=0, tiled=True))
        return lax.psum_scatter(partial_value, "col", scatter_dimension=0, tiled=True)

    def by_rows(vectors):
        partial_value = right_whole(lax.all_gather(vectors, "col", axis=0, tiled=True))
        return lax.psum_scatter(partial_value, "row", scatter_dimension=0, tiled=True)

    begin = lax.all_to_all(start_vectors, "layer", split_axis=0, concat_axis=1, tiled=True)
    result = recurrence(begin, by_columns, by_rows)
    return lax.all_to_all(result, "layer", split_axis=1, concat_axis=0, tiled=True)


def solution(mesh):
    return jax.shard_map(
        local,
        mesh=mesh,
        in_specs=(P("row", "col"), P("row", ("col", "layer")), P(), P()),
        out_specs=P("row", ("col", "layer")),
        check_vma=False,
    )
```

profile of v0, /device:TPU:0, one launch (start us, length us, event | category | flops | bytes accessed | tf_op | source)
XLA Modules:
  0.0 172.7 jit_solution(17839388466532395666)
XLA Ops:
  6.5 3.3 %all-to-all-start = ((bf16[2,32,512]{2,1,0:T(8,128)(2,1)}), bf16[2,32,512]{2,1,0:T(8,128)(2,1)S(1)}, u32[]{:S(2)}, u32[]{:S(2)}) async-start(bf16[2,32,512]{2,1,0:T(8,128)(2,1)} %bitcast.33), calls=%async_computation | async-start | bytes 131072 | tf_op jit(solution)/shard_map/all_to_all | solution.py:46
  9.8 0.0 reduce-scatter.13.cloned.1.call-start
  11.2 0.1 all-to-all-done
  11.2 10.5 %all_gather.12 = bf16[128,1024]{1,0:T(8,128)(2,1)S(1)} all-gather(bf16[32,1024]{1,0:T(8,128)(2,1)S(1)} %bitcast.27), channel_id=1, replica_groups=mesh['row'=4,'col'=4,'layer'=2] {'row'}, dimensions={0}, use_global_device_ids=true | all-gather | bytes 327680 | tf_op jit(solution)/shard_map/all_gather | solution.py:39
  21.7 2.4 %divide_convert_fusion = bf16[1024,1024]{1,0:T(8,128)(2,1)S(1)} fusion(bf16[1024,1024]{1,0:T(8,128)(2,1)} %param.4, f32[]{:T(128)} %bitcast.1, f32[]{:T(128)} %bitcast, s32[1024]{0:T(1024)S(1)} %get-tuple-element.5, s32[1024]{0:T(1024)S(1)} %get-tuple-element.6), kind=kLoop, calls=%fused_computation | loop fusion | flops 6291456 | bytes 4202504 | tf_op jit(solution)/shard_map/convert_element_type | solution.py:12
  24.1 0.7 convolution_bitcast_fusion
  24.8 1.0 copy.28
  25.8 0.0 reduce-scatter.13.cloned.1.call-update
  25.9 0.0 reduce-scatter.15.cloned.1.call-start
  25.9 22.3 %reduce-scatter.13.cloned.1.call-done = f32[32,1024]{1,0:T(8,128)} async-done(((f32[128,1024]{1,0:T(8,128)}), f32[32,1024]{1,0:T(8,128)}) %reduce-scatter.13.cloned.1.call-update) | async-done | bytes 131088 | tf_op jit(solution)/shard_map/reduce_scatter | solution.py:40
  48.2 0.9 convert_element_type.30
  49.1 13.9 %all_gather.13 = bf16[128,1024]{1,0:T(8,128)(2,1)S(1)} all-gather(bf16[32,1024]{1,0:T(8,128)(2,1)S(1)} %convert_element_type.30), channel_id=1, replica_groups=mesh['row'=4,'col'=4,'layer'=2] {'col'}, dimensions={0}, use_global_device_ids=true | all-gather | bytes 327680 | tf_op jit(solution)/shard_map/all_gather | solution.py:43
  63.0 1.2 fusion
  64.2 0.0 reduce-scatter.15.cloned.1.call-update
  64.2 0.0 copy-start
  64.2 0.0 reduce-scatter.17.cloned.1.call-start
  64.3 23.3 %reduce-scatter.15.cloned.1.call-done = f32[32,1024]{1,0:T(8,128)} async-done(((f32[128,1024]{1,0:T(8,128)}), f32[32,1024]{1,0:T(8,128)}) %reduce-scatter.15.cloned.1.call-update) | async-done | bytes 131088 | tf_op jit(solution)/shard_map/reduce_scatter | solution.py:44
  87.5 0.9 subtract_convert_fusion.2
  88.5 9.2 %all_gather.14 = bf16[128,1024]{1,0:T(8,128)(2,1)S(1)} all-gather(bf16[32,1024]{1,0:T(8,128)(2,1)S(1)} %subtract_convert_fusion.2), channel_id=1, replica_groups=mesh['row'=4,'col'=4,'layer'=2] {'row'}, dimensions={0}, use_global_device_ids=true | all-gather | bytes 327680 | tf_op jit(solution)/shard_map/all_gather | solution.py:39
  97.7 1.6 fusion.1
  99.3 0.0 reduce-scatter.17.cloned.1.call-update
  99.3 0.0 reduce-scatter.19.cloned.1.call-start
  99.4 22.0 %reduce-scatter.17.cloned.1.call-done = f32[32,1024]{1,0:T(8,128)} async-done(((f32[128,1024]{1,0:T(8,128)}), f32[32,1024]{1,0:T(8,128)}) %reduce-scatter.17.cloned.1.call-update) | async-done | bytes 131088 | tf_op jit(solution)/shard_map/reduce_scatter | solution.py:40
  121.4 0.0 copy-done
  121.4 0.9 subtract_convert_fusion.1
  122.3 13.8 %all_gather.15 = bf16[128,1024]{1,0:T(8,128)(2,1)S(1)} all-gather(bf16[32,1024]{1,0:T(8,128)(2,1)S(1)} %subtract_convert_fusion.1), channel_id=1, replica_groups=mesh['row'=4,'col'=4,'layer'=2] {'col'}, dimensions={0}, use_global_device_ids=true | all-gather | bytes 327680 | tf_op jit(solution)/shard_map/all_gather | solution.py:43
  136.1 1.2 fusion.2
  137.3 0.0 reduce-scatter.19.cloned.1.call-update
  137.4 23.4 %reduce-scatter.19.cloned.1.call-done = f32[32,1024]{1,0:T(8,128)} async-done(((f32[128,1024]{1,0:T(8,128)}), f32[32,1024]{1,0:T(8,128)}) %reduce-scatter.19.cloned.1.call-update) | async-done | bytes 131088 | tf_op jit(solution)/shard_map/reduce_scatter | solution.py:44
  160.8 0.9 subtract_convert_fusion
  161.7 3.8 %all_to_all.38 = bf16[32,2,512]{2,0,1:T(8,128)(2,1)S(1)} all-to-all(bf16[32,2,512]{2,0,1:T(8,128)(2,1)S(1)} %bitcast.30), channel_id=1, replica_groups=mesh['row'=4,'col'=4,'layer'=2] {'layer'}, dimensions={1} | all-to-all | bytes 131072 | tf_op jit(solution)/shard_map/all_to_all | solution.py:48
  165.5 0.6 copy.43
  (3 shorter events, 0.0 us)
Async XLA Ops:
  6.5 4.7 %all-to-all-start = ((bf16[2,32,512]{2,1,0:T(8,128)(2,1)}), bf16[2,32,512]{2,1,0:T(8,128)(2,1)S(1)}, u32[]{:S(2)}, u32[]{:S(2)}) async-start(bf16[2,32,512]{2,1,0:T(8,128)(2,1)} %bitcast.33), calls=%async_computation | async-start | bytes 131072 | tf_op jit(solution)/shard_map/all_to_all | solution.py:46
  9.8 38.3 %reduce-scatter.13.cloned.1.call-start = ((), (), s32[]{:S(2)}) async-start(), calls=%async_computation.6 | async-start | bytes 655360 | tf_op jit(solution)/shard_map/reduce_scatter | solution.py:40
  25.9 61.7 %reduce-scatter.15.cloned.1.call-start = ((), (), s32[]{:S(2)}) async-start(), calls=%async_computation.7 | async-start | bytes 655360 | tf_op jit(solution)/shard_map/reduce_scatter | solution.py:44
  64.2 57.2 %copy-start = (f32[32,1024]{1,0:T(8,128)S(1)}, f32[32,1024]{1,0:T(8,128)}, u32[]{:S(2)}) copy-start(f32[32,1024]{1,0:T(8,128)} %reduce-scatter.13.cloned.1.call-done) | copy-start | bytes 393220
  64.2 57.1 %reduce-scatter.17.cloned.1.call-start = ((), (), s32[]{:S(2)}) async-start(), calls=%async_computation.8 | async-start | bytes 655360 | tf_op jit(solution)/shard_map/reduce_scatter | solution.py:40
  99.3 61.4 %reduce-scatter.19.cloned.1.call-start = ((), (), s32[]{:S(2)}) async-start(), calls=%async_computation.9 | async-start | bytes 655360 | tf_op jit(solution)/shard_map/reduce_scatter | solution.py:44
Sparse Core Ops, SparseCore 0:
  26.0 22.1 reduce-scatter.12
  64.3 23.1 reduce-scatter.14
  99.5 21.8 reduce-scatter.16
  137.5 23.2 reduce-scatter.18
where the time goes:
time: 173 us
  waiting for transfers between devices  91 us (53%)
  blocking collectives  51.1 us (30%)
  between operations  14.5 us (8%)
  other arithmetic  6.09 us (4%)
  matrix products  4.82 us (3%)
  starting transfers between devices  3.46 us (2%)
    reduce_scatter x2, waiting for transfers between devices, by_rows(): lax.psum_scatter(partial_value, 'row', scatter_dimension=0, tiled=True)  46.7 us
    reduce_scatter x2, waiting for transfers between devices, by_columns(): lax.psum_scatter(partial_value, 'col', scatter_dimension=0, tiled=True)  44.2 us
    all_gather x2, blocking collectives, by_rows(): lax.all_gather(vectors, 'col', axis=0, tiled=True)  27.7 us
    all_gather x2, blocking collectives, by_columns(): lax.all_gather(vectors, 'row', axis=0, tiled=True)  19.7 us
    unnamed x3, matrix products  4.12 us
    all_to_all x1, blocking collectives, local(): lax.all_to_all(result, 'layer', split_axis=1, concat_axis=0, tiled=True)  3.79 us
  transfers between devices with their start and end apart: 5, of which 5 were waited for; matrix products, arithmetic and copies ran while one was open for 0% of the time, Pallas kernels for 0%

commit v1 on v0

--- a/solution.py
+++ b/solution.py
@@ -1,7 +1,16 @@
+import functools
+import math
+
 import jax
 import jax.numpy as jnp
 from jax import lax
+from jax.experimental import pallas as pl
+from jax.experimental.pallas import tpu as pltpu
 from jax.sharding import PartitionSpec as P
+
+
+MIXED = (0, 3, 1, 2)
+SIDE = len(MIXED)
 
 
 def make_shifted(block, first_row, first_col, centre, half_width):
@@ -17,6 +26,107 @@
     second = (2.0 * by_rows(first) - begin.astype(jnp.float32)).astype(jnp.bfloat16)
     third = (2.0 * by_columns(second) - first.astype(jnp.float32)).astype(jnp.bfloat16)
     return (2.0 * by_rows(third) - second.astype(jnp.float32)).astype(jnp.bfloat16)
+
+
+def shift_kernel(rows, block_ref, low_ref, high_ref, whole_ref, turned_ref):
+    height, width = block_ref.shape
+    low, high = low_ref[...], high_ref[...]
+    centre = (low + high) * 0.5
+    scale = 1.0 / ((high - low) * 0.5)
+    offset = lax.axis_index("row") * height - lax.axis_index("col") * width
+    gap = lax.broadcasted_iota(jnp.int32, (rows, width), 1) - lax.broadcasted_iota(jnp.int32, (rows, width), 0)
+    for first in range(0, height, rows):
+        entries = block_ref[pl.ds(first, rows), :].astype(jnp.float32)
+        diagonal = jnp.where(gap == offset + first, centre, 0.0)
+        shifted = ((entries - diagonal) * scale).astype(jnp.bfloat16)
+        whole_ref[pl.ds(first, rows), :] = shifted
+        turned_ref[:, pl.ds(first, rows)] = shifted.T
+
+
+def both_shifted(block, cut_low, cut_high):
+    height, width = block.shape
+    vmem = pl.BlockSpec(memory_space=pltpu.VMEM)
+    return pl.pallas_call(
+        functools.partial(shift_kernel, math.gcd(height, 128)),
+        out_shape=[jax.ShapeDtypeStruct(shape, block.dtype) for shape in ((height, width), (width, height))],
+        in_specs=[vmem] * 3,
+        out_specs=[vmem] * 2,
+        cost_estimate=pl.CostEstimate(flops=4 * block.size, bytes_accessed=6 * block.size, transcendentals=0),
+        compiler_params=pltpu.CompilerParams(vmem_limit_bytes=16 * block.size),
+        name="shift",
+    )(block, cut_low.reshape(1, 1), cut_high.reshape(1, 1))
+
+
+def total(pieces):
+    return sum(piece.astype(jnp.float32) for piece in pieces)
+
+
+def local_direct(hamiltonian, start_vectors, cut_low, cut_high):
+    col, layer = lax.axis_index("col"), lax.axis_index("layer")
+    half, entries = start_vectors.shape[0] // 2, hamiltonian.shape[1] // 2
+    swap = [(0, 1), (1, 0)]
+    steps = range(1, SIDE)
+    unmixed = [MIXED.index(step) for step in range(SIDE)]
+    mixed_col = sum(jnp.where(col == c, MIXED[c], 0) for c in range(SIDE))
+
+    def by_columns(panel):
+        return jnp.dot(panel, turned, preferred_element_type=jnp.float32)
+
+    def by_rows(panel):
+        return jnp.dot(panel, whole, preferred_element_type=jnp.float32)
+
+    def picked(pieces, index):
+        return lax.dynamic_index_in_dim(jnp.stack(pieces), index, 0, False)
+
+    def partner(value, axis, step):
+        return lax.ppermute(value, axis, [(i, i ^ step) for i in range(SIDE)])
+
+    def crossed(value, step):
+        pairs = []
+        for r in range(SIDE):
+            for c in range(SIDE):
+                for l in range(2):
+                    away = MIXED[c] ^ MIXED[step]
+                    pairs.append(((r * SIDE + c) * 2 + l, ((r ^ away) * SIDE + c) * 2 + (l if away else 1 - l)))
+        return lax.ppermute(value, ("row", "col", "layer"), pairs)
+
+    def product(value, axis_in, axis_out, times, table):
+        got = [value] + [partner(value, axis_in, step) for step in steps]
+        sent = [partner(times(got[step]).astype(jnp.bfloat16), axis_out, table[step]) for step in steps]
+        own = lax.optimization_barrier(times(value))
+        return got, total([own] + sent)
+
+    kept = lax.dynamic_slice_in_dim(start_vectors, layer * half, half, 0)
+    other = lax.ppermute(start_vectors, "layer", swap)
+    kept, other = lax.optimization_barrier((kept, other))
+    other = lax.dynamic_slice_in_dim(other, layer * half, half, 0)
+    begin = jnp.where(layer == 0, jnp.concatenate([kept, other], 1), jnp.concatenate([other, kept], 1))
+    begin, hamiltonian = lax.optimization_barrier((begin, hamiltonian))
+    whole, turned = both_shifted(hamiltonian, cut_low, cut_high)
+
+    gathered = [begin] + [partner(begin, "row", step) for step in steps]
+    panel = [picked(gathered, mixed_col ^ MIXED[step]) for step in range(SIDE)]
+    values = jnp.split(by_columns(jnp.concatenate(panel)), SIDE)
+    sent = [partner(values[step].astype(jnp.bfloat16), "col", step) for step in steps]
+    first = total([values[0]] + sent).astype(jnp.bfloat16)
+
+    _, second = product(first, "col", "row", by_rows, MIXED)
+    second = (2.0 * second - panel[0].astype(jnp.float32)).astype(jnp.bfloat16)
+    seconds, third = product(second, "row", "col", by_columns, unmixed)
+    third = (2.0 * third - first.astype(jnp.float32)).astype(jnp.bfloat16)
+
+    gathered = [third] + [partner(third, "col", step) for step in steps]
+    result = 0.0
+    for step in range(SIDE):
+        value = by_rows(gathered[step])
+        back = crossed(value.astype(jnp.bfloat16), step)
+        result += jnp.where(col == step, value, back.astype(jnp.float32))
+    result = (2.0 * result - picked(seconds, mixed_col).astype(jnp.float32)).astype(jnp.bfloat16)
+
+    kept = lax.dynamic_slice_in_dim(result, layer * entries, entries, 1)
+    given = lax.dynamic_slice_in_dim(result, (1 - layer) * entries, entries, 1)
+    other = lax.ppermute(given, "layer", swap)
+    return jnp.where(layer == 0, jnp.concatenate([kept, other]), jnp.concatenate([other, kept]))
 
 
 def local(hamiltonian, start_vectors, cut_low, cut_high):
@@ -49,8 +159,13 @@
 
 
 def solution(mesh):
+    direct = mesh.shape["row"] == SIDE and mesh.shape["col"] == SIDE and mesh.shape["layer"] == 2
+
+    def body(*args):
+        return local_direct(*args) if direct else local(*args)
+
     return jax.shard_map(
-        local,
+        body,
         mesh=mesh,
         in_specs=(P("row", "col"), P("row", ("col", "layer")), P(), P()),
         out_specs=P("row", ("col", "layer")),

time: 173 us -> 69.9 us (0.40)
  waiting for transfers between devices: 91 us -> 24.2 us
  blocking collectives: 51.1 us -> 0 us
  starting transfers between devices: 3.46 us -> 33.6 us
  between operations: 14.5 us -> 1.44 us
  other arithmetic: 6.09 us -> 0.95 us
    reduce_scatter x4 -> x0, waiting for transfers between devices: 90.9 us -> none  [the longest x2 46.7 us: by_rows(): lax.psum_scatter(partial_value, 'row', scatter_dimension=0, tiled=True)]
    all_gather x4 -> x0, blocking collectives: 47.3 us -> none  [the longest x2 27.7 us: by_rows(): lax.all_gather(vectors, 'col', axis=0, tiled=True)]
    ppermute x0 -> x27, starting transfers between devices: none -> 33.6 us  [the longest x21 29.3 us: partner(): return lax.ppermute(value, axis, [(i, i ^ step) for i in range(SIDE)])]
    ppermute x0 -> x27, waiting for transfers between devices: none -> 24.2 us  [the longest x21 19.2 us: partner(): return lax.ppermute(value, axis, [(i, i ^ step) for i in range(SIDE)])]
    convert_element_type x5 -> x4, other arithmetic: 6.09 us -> 0.25 us  [the longest x1 0.12 us: local_direct(): (2.0 * result - picked(seconds, mixed_col).astype(jnp.float32)).astype(jn...]
    dot_general x1 -> x13, matrix products: 0.71 us -> 6.02 us  [the longest x8 3.72 us: by_rows(): return jnp.dot(panel, whole, preferred_element_type=jnp.float32)]
    unnamed x3 -> x0, matrix products: 4.12 us -> none
    all_to_all x1 -> x0, blocking collectives: 3.79 us -> none  [local(): lax.all_to_all(result, 'layer', split_axis=1, concat_axis=0, tiled=True)]
  transfers between devices with their start and end apart: 5 -> 27, of which waited for: 5 -> 15; matrix products, arithmetic and copies ran while one was open for 0% -> 9% of each run, Pallas kernels for 0% -> 2%
where the time goes in v1:
time: 69.9 us; the launch traced here: 69.7 us
  starting transfers between devices  33.6 us (48%)
  waiting for transfers between devices  24.2 us (35%)
  matrix products  6.02 us (9%)
  local copies, waits for them, and re-layouts  2.41 us (3%)
  between operations  1.44 us (2%)
  Pallas kernels  1.12 us (2%)
  other arithmetic  0.95 us (1%)
    ppermute x21, starting transfers between devices, partner(): return lax.ppermute(value, axis, [(i, i ^ step) for i in range(SIDE)])  29.3 us
    ppermute x21, waiting for transfers between devices, partner(): return lax.ppermute(value, axis, [(i, i ^ step) for i in range(SIDE)])  19.2 us
    ppermute x4, starting transfers between devices, crossed(): return lax.ppermute(value, ('row', 'col', 'layer'), pairs)  3.77 us
    dot_general x8, matrix products, by_rows(): return jnp.dot(panel, whole, preferred_element_type=jnp.float32)  3.72 us
    ppermute x4, waiting for transfers between devices, crossed(): return lax.ppermute(value, ('row', 'col', 'layer'), pairs)  3.45 us
    dot_general x5, matrix products, by_columns(): return jnp.dot(panel, turned, preferred_element_type=jnp.float32)  2.3 us
    unnamed x2, local copies, waits for them, and re-layouts  1.59 us
  transfers between devices with their start and end apart: 27, of which 15 were waited for; matrix products, arithmetic and copies ran while one was open for 9% of the time, Pallas kernels for 2%

profile of v1, /device:TPU:0, one launch (start us, length us, event | category | flops | bytes accessed | tf_op | source)
XLA Modules:
  0.0 69.7 jit_solution(4954270758584204098)
XLA Ops:
  0.5 0.8 %constant_dynamic-slice_fusion.3 = bf16[32,512]{1,0:T(8,128)(2,1)S(1)} fusion(bf16[64,512]{1,0:T(8,128)(2,1)} %param.5, s32[]{:T(128)S(6)} %select_n.80), kind=kLoop, calls=%fused_computation.40 | loop fusion | bytes 65540 | tf_op jit(solution)/shard_map/dynamic_slice | solution.py:99
  1.6 3.8 %collective-permute-start.3 = (bf16[32,1024]{1,0:T(8,128)(2,1)S(1)}, bf16[32,1024]{1,0:T(8,128)(2,1)S(1)}, u32[]{:S(2)}, u32[]{:S(2)}) collective-permute-start(bf16[32,1024]{1,0:T(8,128)(2,1)S(1)} %maximum_select_fusion), channel_id=1, source_target_pairs={{0,24},{8,16},{16,8},{24,0},{1,25},{9,17},{17,9},{25,1},{2,26},{10... | collective-permute-start | bytes 196616 | tf_op jit(solution)/shard_map/ppermute | solution.py:82
  7.4 1.6 %copy-done = bf16[1024,1024]{1,0:T(8,128)(2,1)S(1)} copy-done((bf16[1024,1024]{1,0:T(8,128)(2,1)S(1)}, bf16[1024,1024]{1,0:T(8,128)(2,1)}, u32[]{:S(2)}) %copy-start) | copy-done | bytes 2097176
  9.0 1.1 %shift.1 = (bf16[1024,1024]{1,0:T(8,128)(2,1)S(1)}, bf16[1024,1024]{1,0:T(8,128)(2,1)S(1)}) custom-call(bf16[1024,1024]{1,0:T(8,128)(2,1)S(1)} %copy-done, f32[1,1]{1,0:T(1,128)} %bitcast.48.low_ref, f32[1,1]{1,0:T(1,128)} %bitcast.49.high_ref), custom_call_target="tpu_custom_call" | custom-call | flops 4194304 | bytes 6291456 | tf_op jit(solution)/shard_map/shift/pallas_call | solution.py:49
  10.8 4.0 %collective-permute-start.6 = (bf16[32,1024]{1,0:T(8,128)(2,1)S(1)}, bf16[32,1024]{1,0:T(8,128)(2,1)S(1)}, u32[]{:S(2)}, u32[]{:S(2)}) collective-permute-start(bf16[32,1024]{1,0:T(8,128)(2,1)S(1)} %get-tuple-element.18), channel_id=1, source_target_pairs={{0,6},{2,4},{4,2},{6,0},{1,7},{3,5},{5,3},{7,1},{8,14},{10,12},{12... | collective-permute-start | bytes 196616 | tf_op jit(solution)/shard_map/ppermute | solution.py:82
  15.4 2.4 %collective-permute-done.6 = bf16[32,1024]{1,0:T(8,128)(2,1)S(1)} collective-permute-done((bf16[32,1024]{1,0:T(8,128)(2,1)S(1)}, bf16[32,1024]{1,0:T(8,128)(2,1)S(1)}, u32[]{:S(2)}, u32[]{:S(2)}) %collective-permute-start.6) | collective-permute-done | bytes 65568 | tf_op jit(solution)/shard_map/ppermute | solution.py:82
  17.8 2.2 %collective-permute-done.5 = bf16[32,1024]{1,0:T(8,128)(2,1)S(1)} collective-permute-done((bf16[32,1024]{1,0:T(8,128)(2,1)S(1)}, bf16[32,1024]{1,0:T(8,128)(2,1)S(1)}, u32[]{:S(2)}, u32[]{:S(2)}) %collective-permute-start.5) | collective-permute-done | bytes 65568 | tf_op jit(solution)/shard_map/ppermute | solution.py:82
  20.1 2.6 %collective-permute-start.11 = (bf16[32,1024]{1,0:T(8,128)(2,1)S(1)}, bf16[32,1024]{1,0:T(8,128)(2,1)S(1)}, u32[]{:S(2)}, u32[]{:S(2)}) collective-permute-start(bf16[32,1024]{1,0:T(8,128)(2,1)S(1)} %fusion.10), channel_id=1, source_target_pairs={{0,6},{2,4},{4,2},{6,0},{1,7},{3,5},{5,3},{7,1},{8,14},{10,12},{12... | collective-permute-start | bytes 196616 | tf_op jit(solution)/shard_map/ppermute | solution.py:82
  22.7 1.9 %collective-permute-start.7 = (bf16[32,1024]{1,0:T(8,128)(2,1)S(1)}, bf16[32,1024]{1,0:T(8,128)(2,1)S(1)}, u32[]{:S(2)}, u32[]{:S(2)}) collective-permute-start(bf16[32,1024]{1,0:T(8,128)(2,1)S(1)} %fusion.10), channel_id=1, source_target_pairs={{0,2},{2,0},{4,6},{6,4},{1,3},{3,1},{5,7},{7,5},{8,10},{10,8},{12,... | collective-permute-start | bytes 196616 | tf_op jit(solution)/shard_map/ppermute | solution.py:82
  24.6 1.9 %collective-permute-done.11 = bf16[32,1024]{1,0:T(8,128)(2,1)S(1)} collective-permute-done((bf16[32,1024]{1,0:T(8,128)(2,1)S(1)}, bf16[32,1024]{1,0:T(8,128)(2,1)S(1)}, u32[]{:S(2)}, u32[]{:S(2)}) %collective-permute-start.11) | collective-permute-done | bytes 65568 | tf_op jit(solution)/shard_map/ppermute | solution.py:82
  26.9 1.5 %collective-permute-start.12 = (bf16[32,1024]{1,0:T(8,128)(2,1)S(1)}, bf16[32,1024]{1,0:T(8,128)(2,1)S(1)}, u32[]{:S(2)}, u32[]{:S(2)}) collective-permute-start(bf16[32,1024]{1,0:T(8,128)(2,1)S(1)} %convolution_convert_fusion.3), channel_id=1, source_target_pairs={{0,16},{8,24},{16,0},{24,8},{1,17},{9,25},{17,1},{25,9},{2,18},{10... | collective-permute-start | bytes 196616 | tf_op jit(solution)/shard_map/ppermute | solution.py:82
  28.9 1.5 %collective-permute-start.10 = (bf16[32,1024]{1,0:T(8,128)(2,1)S(1)}, bf16[32,1024]{1,0:T(8,128)(2,1)S(1)}, u32[]{:S(2)}, u32[]{:S(2)}) collective-permute-start(bf16[32,1024]{1,0:T(8,128)(2,1)S(1)} %convolution_convert_fusion.4), channel_id=1, source_target_pairs={{0,8},{8,0},{16,24},{24,16},{1,9},{9,1},{17,25},{25,17},{2,10},{10... | collective-permute-start | bytes 196616 | tf_op jit(solution)/shard_map/ppermute | solution.py:82
  30.9 1.1 %collective-permute-start.8 = (bf16[32,1024]{1,0:T(8,128)(2,1)S(1)}, bf16[32,1024]{1,0:T(8,128)(2,1)S(1)}, u32[]{:S(2)}, u32[]{:S(2)}) collective-permute-start(bf16[32,1024]{1,0:T(8,128)(2,1)S(1)} %convolution_convert_fusion.5), channel_id=1, source_target_pairs={{0,24},{8,16},{16,8},{24,0},{1,25},{9,17},{17,9},{25,1},{2,26},{10... | collective-permute-start | bytes 196616 | tf_op jit(solution)/shard_map/ppermute | solution.py:82
  32.5 0.7 %collective-permute-done.10 = bf16[32,1024]{1,0:T(8,128)(2,1)S(1)} collective-permute-done((bf16[32,1024]{1,0:T(8,128)(2,1)S(1)}, bf16[32,1024]{1,0:T(8,128)(2,1)S(1)}, u32[]{:S(2)}, u32[]{:S(2)}) %collective-permute-start.10) | collective-permute-done | bytes 65568 | tf_op jit(solution)/shard_map/ppermute | solution.py:82
  33.2 3.4 %collective-permute-done.8 = bf16[32,1024]{1,0:T(8,128)(2,1)S(1)} collective-permute-done((bf16[32,1024]{1,0:T(8,128)(2,1)S(1)}, bf16[32,1024]{1,0:T(8,128)(2,1)S(1)}, u32[]{:S(2)}, u32[]{:S(2)}) %collective-permute-start.8) | collective-permute-done | bytes 65568 | tf_op jit(solution)/shard_map/ppermute | solution.py:82
  36.6 1.2 %collective-permute-start.17 = (bf16[32,1024]{1,0:T(8,128)(2,1)S(1)}, bf16[32,1024]{1,0:T(8,128)(2,1)S(1)}, u32[]{:S(2)}, u32[]{:S(2)}) collective-permute-start(bf16[32,1024]{1,0:T(8,128)(2,1)S(1)} %subtract_convert_fusion.1), channel_id=1, source_target_pairs={{0,24},{8,16},{16,8},{24,0},{1,25},{9,17},{17,9},{25,1},{2,26},{10... | collective-permute-start | bytes 196616 | tf_op jit(solution)/shard_map/ppermute | solution.py:82
  37.9 0.7 collective-permute-start.15
  38.5 1.7 %collective-permute-start.13 = (bf16[32,1024]{1,0:T(8,128)(2,1)S(1)}, bf16[32,1024]{1,0:T(8,128)(2,1)S(1)}, u32[]{:S(2)}, u32[]{:S(2)}) collective-permute-start(bf16[32,1024]{1,0:T(8,128)(2,1)S(1)} %subtract_convert_fusion.1), channel_id=1, source_target_pairs={{0,8},{8,0},{16,24},{24,16},{1,9},{9,1},{17,25},{25,17},{2,10},{10... | collective-permute-start | bytes 196616 | tf_op jit(solution)/shard_map/ppermute | solution.py:82
  40.2 1.7 %collective-permute-done.17 = bf16[32,1024]{1,0:T(8,128)(2,1)S(1)} collective-permute-done((bf16[32,1024]{1,0:T(8,128)(2,1)S(1)}, bf16[32,1024]{1,0:T(8,128)(2,1)S(1)}, u32[]{:S(2)}, u32[]{:S(2)}) %collective-permute-start.17) | collective-permute-done | bytes 65568 | tf_op jit(solution)/shard_map/ppermute | solution.py:82
  42.4 1.7 %collective-permute-start.18 = (bf16[32,1024]{1,0:T(8,128)(2,1)S(1)}, bf16[32,1024]{1,0:T(8,128)(2,1)S(1)}, u32[]{:S(2)}, u32[]{:S(2)}) collective-permute-start(bf16[32,1024]{1,0:T(8,128)(2,1)S(1)} %convolution_convert_fusion), channel_id=1, source_target_pairs={{0,2},{2,0},{4,6},{6,4},{1,3},{3,1},{5,7},{7,5},{8,10},{10,8},{12,... | collective-permute-start | bytes 196616 | tf_op jit(solution)/shard_map/ppermute | solution.py:82
  45.6 1.3 %collective-permute-start.14 = (bf16[32,1024]{1,0:T(8,128)(2,1)S(1)}, bf16[32,1024]{1,0:T(8,128)(2,1)S(1)}, u32[]{:S(2)}, u32[]{:S(2)}) collective-permute-start(bf16[32,1024]{1,0:T(8,128)(2,1)S(1)} %convolution_convert_fusion.2), channel_id=1, source_target_pairs={{0,4},{2,6},{4,0},{6,2},{1,5},{3,7},{5,1},{7,3},{8,12},{10,14},{12... | collective-permute-start | bytes 196616 | tf_op jit(solution)/shard_map/ppermute | solution.py:82
  47.3 3.5 %collective-permute-done.16 = bf16[32,1024]{1,0:T(8,128)(2,1)S(1)} collective-permute-done((bf16[32,1024]{1,0:T(8,128)(2,1)S(1)}, bf16[32,1024]{1,0:T(8,128)(2,1)S(1)}, u32[]{:S(2)}, u32[]{:S(2)}) %collective-permute-start.16) | collective-permute-done | bytes 65568 | tf_op jit(solution)/shard_map/ppermute | solution.py:82
  50.8 2.0 %collective-permute-done.14 = bf16[32,1024]{1,0:T(8,128)(2,1)S(1)} collective-permute-done((bf16[32,1024]{1,0:T(8,128)(2,1)S(1)}, bf16[32,1024]{1,0:T(8,128)(2,1)S(1)}, u32[]{:S(2)}, u32[]{:S(2)}) %collective-permute-start.14) | collective-permute-done | bytes 65568 | tf_op jit(solution)/shard_map/ppermute | solution.py:82
  52.9 2.1 %collective-permute-start.24 = (bf16[32,1024]{1,0:T(8,128)(2,1)S(1)}, bf16[32,1024]{1,0:T(8,128)(2,1)S(1)}, u32[]{:S(2)}, u32[]{:S(2)}) collective-permute-start(bf16[32,1024]{1,0:T(8,128)(2,1)S(1)} %subtract_convert_fusion), channel_id=1, source_target_pairs={{0,6},{2,4},{4,2},{6,0},{1,7},{3,5},{5,3},{7,1},{8,14},{10,12},{12... | collective-permute-start | bytes 196616 | tf_op jit(solution)/shard_map/ppermute | solution.py:82
  55.1 2.3 %collective-permute-start.20 = (bf16[32,1024]{1,0:T(8,128)(2,1)S(1)}, bf16[32,1024]{1,0:T(8,128)(2,1)S(1)}, u32[]{:S(2)}, u32[]{:S(2)}) collective-permute-start(bf16[32,1024]{1,0:T(8,128)(2,1)S(1)} %subtract_convert_fusion), channel_id=1, source_target_pairs={{0,2},{2,0},{4,6},{6,4},{1,3},{3,1},{5,7},{7,5},{8,10},{10,8},{12,... | collective-permute-start | bytes 196616 | tf_op jit(solution)/shard_map/ppermute | solution.py:82
  57.9 1.2 %collective-permute-done.24 = bf16[32,1024]{1,0:T(8,128)(2,1)S(1)} collective-permute-done((bf16[32,1024]{1,0:T(8,128)(2,1)S(1)}, bf16[32,1024]{1,0:T(8,128)(2,1)S(1)}, u32[]{:S(2)}, u32[]{:S(2)}) %collective-permute-start.24) | collective-permute-done | bytes 65568 | tf_op jit(solution)/shard_map/ppermute | solution.py:82
  59.5 1.3 %collective-permute-start.25 = (bf16[32,1024]{1,0:T(8,128)(2,1)S(1)}, bf16[32,1024]{1,0:T(8,128)(2,1)S(1)}, u32[]{:S(2)}, u32[]{:S(2)}) collective-permute-start(bf16[32,1024]{1,0:T(8,128)(2,1)S(1)} %get-tuple-element.28), channel_id=1, source_target_pairs={{0,16},{1,17},{2,10},{3,11},{4,28},{5,29},{6,7},{7,6},{8,24},{9,25... | collective-permute-start | bytes 196616 | tf_op jit(solution)/shard_map/ppermute | solution.py:91
  61.3 0.7 collective-permute-start.23
  62.5 1.7 %collective-permute-start.21 = (bf16[32,1024]{1,0:T(8,128)(2,1)S(1)}, bf16[32,1024]{1,0:T(8,128)(2,1)S(1)}, u32[]{:S(2)}, u32[]{:S(2)}) collective-permute-start(bf16[32,1024]{1,0:T(8,128)(2,1)S(1)} %get-tuple-element.32), channel_id=1, source_target_pairs={{0,24},{1,25},{2,3},{3,2},{4,20},{5,21},{6,14},{7,15},{8,16},{9,17... | collective-permute-start | bytes 196616 | tf_op jit(solution)/shard_map/ppermute | solution.py:91
  64.2 1.4 %collective-permute-done.23 = bf16[32,1024]{1,0:T(8,128)(2,1)S(1)} collective-permute-done((bf16[32,1024]{1,0:T(8,128)(2,1)S(1)}, bf16[32,1024]{1,0:T(8,128)(2,1)S(1)}, u32[]{:S(2)}, u32[]{:S(2)}) %collective-permute-start.23) | collective-permute-done | bytes 65568 | tf_op jit(solution)/shard_map/ppermute | solution.py:91
  65.6 2.0 %collective-permute-done.21 = bf16[32,1024]{1,0:T(8,128)(2,1)S(1)} collective-permute-done((bf16[32,1024]{1,0:T(8,128)(2,1)S(1)}, bf16[32,1024]{1,0:T(8,128)(2,1)S(1)}, u32[]{:S(2)}, u32[]{:S(2)}) %collective-permute-start.21) | collective-permute-done | bytes 65568 | tf_op jit(solution)/shard_map/ppermute | solution.py:91
  67.9 1.2 %collective-permute-done.26 = bf16[32,512]{1,0:T(8,128)(2,1)S(1)} collective-permute-done((bf16[32,512]{1,0:T(8,128)(2,1)S(1)}, bf16[32,512]{1,0:T(8,128)(2,1)S(1)}, u32[]{:S(2)}, u32[]{:S(2)}) %collective-permute-start.26) | collective-permute-done | bytes 32800 | tf_op jit(solution)/shard_map/ppermute | solution.py:128
  (50 shorter events, 10.0 us)
Async XLA Ops:
  0.0 1.6 %collective-permute-start = (bf16[64,512]{1,0:T(8,128)(2,1)}, bf16[64,512]{1,0:T(8,128)(2,1)S(1)}, u32[]{:S(2)}, u32[]{:S(2)}) collective-permute-start(bf16[64,512]{1,0:T(8,128)(2,1)} %param.5), channel_id=1, source_target_pairs={{0,1},{1,0},{2,3},{3,2},{4,5},{5,4},{6,7},{7,6},{8,9},{9,8},{10,11... | collective-permute-start | bytes 196616 | tf_op jit(solution)/shard_map/ppermute | solution.py:100
  1.6 8.5 %collective-permute-start.3 = (bf16[32,1024]{1,0:T(8,128)(2,1)S(1)}, bf16[32,1024]{1,0:T(8,128)(2,1)S(1)}, u32[]{:S(2)}, u32[]{:S(2)}) collective-permute-start(bf16[32,1024]{1,0:T(8,128)(2,1)S(1)} %maximum_select_fusion), channel_id=1, source_target_pairs={{0,24},{8,16},{16,8},{24,0},{1,25},{9,17},{17,9},{25,1},{2,26},{10... | collective-permute-start | bytes 196616 | tf_op jit(solution)/shard_map/ppermute | solution.py:82
  5.5 4.7 %collective-permute-start.2 = (bf16[32,1024]{1,0:T(8,128)(2,1)S(1)}, bf16[32,1024]{1,0:T(8,128)(2,1)S(1)}, u32[]{:S(2)}, u32[]{:S(2)}) collective-permute-start(bf16[32,1024]{1,0:T(8,128)(2,1)S(1)} %maximum_select_fusion), channel_id=1, source_target_pairs={{0,16},{8,24},{16,0},{24,8},{1,17},{9,25},{17,1},{25,9},{2,18},{10... | collective-permute-start | bytes 196616 | tf_op jit(solution)/shard_map/ppermute | solution.py:82
  6.0 4.3 %collective-permute-start.1 = (bf16[32,1024]{1,0:T(8,128)(2,1)S(1)}, bf16[32,1024]{1,0:T(8,128)(2,1)S(1)}, u32[]{:S(2)}, u32[]{:S(2)}) collective-permute-start(bf16[32,1024]{1,0:T(8,128)(2,1)S(1)} %maximum_select_fusion), channel_id=1, source_target_pairs={{0,8},{8,0},{16,24},{24,16},{1,9},{9,1},{17,25},{25,17},{2,10},{10... | collective-permute-start | bytes 196616 | tf_op jit(solution)/shard_map/ppermute | solution.py:82
  7.4 1.6 %copy-start = (bf16[1024,1024]{1,0:T(8,128)(2,1)S(1)}, bf16[1024,1024]{1,0:T(8,128)(2,1)}, u32[]{:S(2)}) copy-start(bf16[1024,1024]{1,0:T(8,128)(2,1)} %block_ref) | copy-start | bytes 6291460
  10.8 7.0 %collective-permute-start.6 = (bf16[32,1024]{1,0:T(8,128)(2,1)S(1)}, bf16[32,1024]{1,0:T(8,128)(2,1)S(1)}, u32[]{:S(2)}, u32[]{:S(2)}) collective-permute-start(bf16[32,1024]{1,0:T(8,128)(2,1)S(1)} %get-tuple-element.18), channel_id=1, source_target_pairs={{0,6},{2,4},{4,2},{6,0},{1,7},{3,5},{5,3},{7,1},{8,14},{10,12},{12... | collective-permute-start | bytes 196616 | tf_op jit(solution)/shard_map/ppermute | solution.py:82
  14.8 5.2 %collective-permute-start.5 = (bf16[32,1024]{1,0:T(8,128)(2,1)S(1)}, bf16[32,1024]{1,0:T(8,128)(2,1)S(1)}, u32[]{:S(2)}, u32[]{:S(2)}) collective-permute-start(bf16[32,1024]{1,0:T(8,128)(2,1)S(1)} %get-tuple-element.19), channel_id=1, source_target_pairs={{0,4},{2,6},{4,0},{6,2},{1,5},{3,7},{5,1},{7,3},{8,12},{10,14},{12... | collective-permute-start | bytes 196616 | tf_op jit(solution)/shard_map/ppermute | solution.py:82
  14.8 5.3 %collective-permute-start.4 = (bf16[32,1024]{1,0:T(8,128)(2,1)S(1)}, bf16[32,1024]{1,0:T(8,128)(2,1)S(1)}, u32[]{:S(2)}, u32[]{:S(2)}) collective-permute-start(bf16[32,1024]{1,0:T(8,128)(2,1)S(1)} %get-tuple-element.17), channel_id=1, source_target_pairs={{0,2},{2,0},{4,6},{6,4},{1,3},{3,1},{5,7},{7,5},{8,10},{10,8},{12,... | collective-permute-start | bytes 196616 | tf_op jit(solution)/shard_map/ppermute | solution.py:82
  20.1 6.3 %collective-permute-start.11 = (bf16[32,1024]{1,0:T(8,128)(2,1)S(1)}, bf16[32,1024]{1,0:T(8,128)(2,1)S(1)}, u32[]{:S(2)}, u32[]{:S(2)}) collective-permute-start(bf16[32,1024]{1,0:T(8,128)(2,1)S(1)} %fusion.10), channel_id=1, source_target_pairs={{0,6},{2,4},{4,2},{6,0},{1,7},{3,5},{5,3},{7,1},{8,14},{10,12},{12... | collective-permute-start | bytes 196616 | tf_op jit(solution)/shard_map/ppermute | solution.py:82
  22.7 5.8 %collective-permute-start.9 = (bf16[32,1024]{1,0:T(8,128)(2,1)S(1)}, bf16[32,1024]{1,0:T(8,128)(2,1)S(1)}, u32[]{:S(2)}, u32[]{:S(2)}) collective-permute-start(bf16[32,1024]{1,0:T(8,128)(2,1)S(1)} %fusion.10), channel_id=1, source_target_pairs={{0,4},{2,6},{4,0},{6,2},{1,5},{3,7},{5,1},{7,3},{8,12},{10,14},{12... | collective-permute-start | bytes 196616 | tf_op jit(solution)/shard_map/ppermute | solution.py:82
  22.7 7.7 %collective-permute-start.7 = (bf16[32,1024]{1,0:T(8,128)(2,1)S(1)}, bf16[32,1024]{1,0:T(8,128)(2,1)S(1)}, u32[]{:S(2)}, u32[]{:S(2)}) collective-permute-start(bf16[32,1024]{1,0:T(8,128)(2,1)S(1)} %fusion.10), channel_id=1, source_target_pairs={{0,2},{2,0},{4,6},{6,4},{1,3},{3,1},{5,7},{7,5},{8,10},{10,8},{12,... | collective-permute-start | bytes 196616 | tf_op jit(solution)/shard_map/ppermute | solution.py:82
  26.9 5.6 %collective-permute-start.12 = (bf16[32,1024]{1,0:T(8,128)(2,1)S(1)}, bf16[32,1024]{1,0:T(8,128)(2,1)S(1)}, u32[]{:S(2)}, u32[]{:S(2)}) collective-permute-start(bf16[32,1024]{1,0:T(8,128)(2,1)S(1)} %convolution_convert_fusion.3), channel_id=1, source_target_pairs={{0,16},{8,24},{16,0},{24,8},{1,17},{9,25},{17,1},{25,9},{2,18},{10... | collective-permute-start | bytes 196616 | tf_op jit(solution)/shard_map/ppermute | solution.py:82
  28.9 4.3 %collective-permute-start.10 = (bf16[32,1024]{1,0:T(8,128)(2,1)S(1)}, bf16[32,1024]{1,0:T(8,128)(2,1)S(1)}, u32[]{:S(2)}, u32[]{:S(2)}) collective-permute-start(bf16[32,1024]{1,0:T(8,128)(2,1)S(1)} %convolution_convert_fusion.4), channel_id=1, source_target_pairs={{0,8},{8,0},{16,24},{24,16},{1,9},{9,1},{17,25},{25,17},{2,10},{10... | collective-permute-start | bytes 196616 | tf_op jit(solution)/shard_map/ppermute | solution.py:82
  30.9 5.7 %collective-permute-start.8 = (bf16[32,1024]{1,0:T(8,128)(2,1)S(1)}, bf16[32,1024]{1,0:T(8,128)(2,1)S(1)}, u32[]{:S(2)}, u32[]{:S(2)}) collective-permute-start(bf16[32,1024]{1,0:T(8,128)(2,1)S(1)} %convolution_convert_fusion.5), channel_id=1, source_target_pairs={{0,24},{8,16},{16,8},{24,0},{1,25},{9,17},{17,9},{25,1},{2,26},{10... | collective-permute-start | bytes 196616 | tf_op jit(solution)/shard_map/ppermute | solution.py:82
  36.6 5.3 %collective-permute-start.17 = (bf16[32,1024]{1,0:T(8,128)(2,1)S(1)}, bf16[32,1024]{1,0:T(8,128)(2,1)S(1)}, u32[]{:S(2)}, u32[]{:S(2)}) collective-permute-start(bf16[32,1024]{1,0:T(8,128)(2,1)S(1)} %subtract_convert_fusion.1), channel_id=1, source_target_pairs={{0,24},{8,16},{16,8},{24,0},{1,25},{9,17},{17,9},{25,1},{2,26},{10... | collective-permute-start | bytes 196616 | tf_op jit(solution)/shard_map/ppermute | solution.py:82
  37.9 6.2 %collective-permute-start.15 = (bf16[32,1024]{1,0:T(8,128)(2,1)S(1)}, bf16[32,1024]{1,0:T(8,128)(2,1)S(1)}, u32[]{:S(2)}, u32[]{:S(2)}) collective-permute-start(bf16[32,1024]{1,0:T(8,128)(2,1)S(1)} %subtract_convert_fusion.1), channel_id=1, source_target_pairs={{0,16},{8,24},{16,0},{24,8},{1,17},{9,25},{17,1},{25,9},{2,18},{10... | collective-permute-start | bytes 196616 | tf_op jit(solution)/shard_map/ppermute | solution.py:82
  38.5 6.6 %collective-permute-start.13 = (bf16[32,1024]{1,0:T(8,128)(2,1)S(1)}, bf16[32,1024]{1,0:T(8,128)(2,1)S(1)}, u32[]{:S(2)}, u32[]{:S(2)}) collective-permute-start(bf16[32,1024]{1,0:T(8,128)(2,1)S(1)} %subtract_convert_fusion.1), channel_id=1, source_target_pairs={{0,8},{8,0},{16,24},{24,16},{1,9},{9,1},{17,25},{25,17},{2,10},{10... | collective-permute-start | bytes 196616 | tf_op jit(solution)/shard_map/ppermute | solution.py:82
  42.4 4.9 %collective-permute-start.18 = (bf16[32,1024]{1,0:T(8,128)(2,1)S(1)}, bf16[32,1024]{1,0:T(8,128)(2,1)S(1)}, u32[]{:S(2)}, u32[]{:S(2)}) collective-permute-start(bf16[32,1024]{1,0:T(8,128)(2,1)S(1)} %convolution_convert_fusion), channel_id=1, source_target_pairs={{0,2},{2,0},{4,6},{6,4},{1,3},{3,1},{5,7},{7,5},{8,10},{10,8},{12,... | collective-permute-start | bytes 196616 | tf_op jit(solution)/shard_map/ppermute | solution.py:82
  44.6 6.3 %collective-permute-start.16 = (bf16[32,1024]{1,0:T(8,128)(2,1)S(1)}, bf16[32,1024]{1,0:T(8,128)(2,1)S(1)}, u32[]{:S(2)}, u32[]{:S(2)}) collective-permute-start(bf16[32,1024]{1,0:T(8,128)(2,1)S(1)} %convolution_convert_fusion.1), channel_id=1, source_target_pairs={{0,6},{2,4},{4,2},{6,0},{1,7},{3,5},{5,3},{7,1},{8,14},{10,12},{12... | collective-permute-start | bytes 196616 | tf_op jit(solution)/shard_map/ppermute | solution.py:82
  45.6 7.2 %collective-permute-start.14 = (bf16[32,1024]{1,0:T(8,128)(2,1)S(1)}, bf16[32,1024]{1,0:T(8,128)(2,1)S(1)}, u32[]{:S(2)}, u32[]{:S(2)}) collective-permute-start(bf16[32,1024]{1,0:T(8,128)(2,1)S(1)} %convolution_convert_fusion.2), channel_id=1, source_target_pairs={{0,4},{2,6},{4,0},{6,2},{1,5},{3,7},{5,1},{7,3},{8,12},{10,14},{12... | collective-permute-start | bytes 196616 | tf_op jit(solution)/shard_map/ppermute | solution.py:82
  52.9 6.1 %collective-permute-start.24 = (bf16[32,1024]{1,0:T(8,128)(2,1)S(1)}, bf16[32,1024]{1,0:T(8,128)(2,1)S(1)}, u32[]{:S(2)}, u32[]{:S(2)}) collective-permute-start(bf16[32,1024]{1,0:T(8,128)(2,1)S(1)} %subtract_convert_fusion), channel_id=1, source_target_pairs={{0,6},{2,4},{4,2},{6,0},{1,7},{3,5},{5,3},{7,1},{8,14},{10,12},{12... | collective-permute-start | bytes 196616 | tf_op jit(solution)/shard_map/ppermute | solution.py:82
  55.1 5.8 %collective-permute-start.22 = (bf16[32,1024]{1,0:T(8,128)(2,1)S(1)}, bf16[32,1024]{1,0:T(8,128)(2,1)S(1)}, u32[]{:S(2)}, u32[]{:S(2)}) collective-permute-start(bf16[32,1024]{1,0:T(8,128)(2,1)S(1)} %subtract_convert_fusion), channel_id=1, source_target_pairs={{0,4},{2,6},{4,0},{6,2},{1,5},{3,7},{5,1},{7,3},{8,12},{10,14},{12... | collective-permute-start | bytes 196616 | tf_op jit(solution)/shard_map/ppermute | solution.py:82
  55.1 7.0 %collective-permute-start.20 = (bf16[32,1024]{1,0:T(8,128)(2,1)S(1)}, bf16[32,1024]{1,0:T(8,128)(2,1)S(1)}, u32[]{:S(2)}, u32[]{:S(2)}) collective-permute-start(bf16[32,1024]{1,0:T(8,128)(2,1)S(1)} %subtract_convert_fusion), channel_id=1, source_target_pairs={{0,2},{2,0},{4,6},{6,4},{1,3},{3,1},{5,7},{7,5},{8,10},{10,8},{12,... | collective-permute-start | bytes 196616 | tf_op jit(solution)/shard_map/ppermute | solution.py:82
  57.8 6.4 %collective-permute-start.19 = (bf16[32,1024]{1,0:T(8,128)(2,1)S(1)}, bf16[32,1024]{1,0:T(8,128)(2,1)S(1)}, u32[]{:S(2)}, u32[]{:S(2)}) collective-permute-start(bf16[32,1024]{1,0:T(8,128)(2,1)S(1)} %get-tuple-element.34), channel_id=1, source_target_pairs={{0,1},{1,0},{2,26},{3,27},{4,12},{5,13},{6,22},{7,23},{8,9},{9,8},... | collective-permute-start | bytes 196616 | tf_op jit(solution)/shard_map/ppermute | solution.py:91
  59.5 4.7 %collective-permute-start.25 = (bf16[32,1024]{1,0:T(8,128)(2,1)S(1)}, bf16[32,1024]{1,0:T(8,128)(2,1)S(1)}, u32[]{:S(2)}, u32[]{:S(2)}) collective-permute-start(bf16[32,1024]{1,0:T(8,128)(2,1)S(1)} %get-tuple-element.28), channel_id=1, source_target_pairs={{0,16},{1,17},{2,10},{3,11},{4,28},{5,29},{6,7},{7,6},{8,24},{9,25... | collective-permute-start | bytes 196616 | tf_op jit(solution)/shard_map/ppermute | solution.py:91
  61.3 4.3 %collective-permute-start.23 = (bf16[32,1024]{1,0:T(8,128)(2,1)S(1)}, bf16[32,1024]{1,0:T(8,128)(2,1)S(1)}, u32[]{:S(2)}, u32[]{:S(2)}) collective-permute-start(bf16[32,1024]{1,0:T(8,128)(2,1)S(1)} %get-tuple-element.30), channel_id=1, source_target_pairs={{0,8},{1,9},{2,18},{3,19},{4,5},{5,4},{6,30},{7,31},{8,0},{9,1},{1... | collective-permute-start | bytes 196616 | tf_op jit(solution)/shard_map/ppermute | solution.py:91
  62.5 5.2 %collective-permute-start.21 = (bf16[32,1024]{1,0:T(8,128)(2,1)S(1)}, bf16[32,1024]{1,0:T(8,128)(2,1)S(1)}, u32[]{:S(2)}, u32[]{:S(2)}) collective-permute-start(bf16[32,1024]{1,0:T(8,128)(2,1)S(1)} %get-tuple-element.32), channel_id=1, source_target_pairs={{0,24},{1,25},{2,3},{3,2},{4,20},{5,21},{6,14},{7,15},{8,16},{9,17... | collective-permute-start | bytes 196616 | tf_op jit(solution)/shard_map/ppermute | solution.py:91
  67.8 1.3 %collective-permute-start.26 = (bf16[32,512]{1,0:T(8,128)(2,1)S(1)}, bf16[32,512]{1,0:T(8,128)(2,1)S(1)}, u32[]{:S(2)}, u32[]{:S(2)}) collective-permute-start(bf16[32,512]{1,0:T(8,128)(2,1)S(1)} %get-tuple-element.25), channel_id=1, source_target_pairs={{0,1},{1,0},{2,3},{3,2},{4,5},{5,4},{6,7},{7,6},{8,9},{9,8},{10,11... | collective-permute-start | bytes 98312 | tf_op jit(solution)/shard_map/ppermute | solution.py:128

commit v2 on v1

--- a/solution.py
+++ b/solution.py
@@ -90,9 +90,16 @@
                     pairs.append(((r * SIDE + c) * 2 + l, ((r ^ away) * SIDE + c) * 2 + (l if away else 1 - l)))
         return lax.ppermute(value, ("row", "col", "layer"), pairs)
 
-    def product(value, axis_in, axis_out, times, table):
+    def together(times, pieces):
+        return jnp.split(times(jnp.concatenate(pieces)), len(pieces))
+
+    def product(value, axis_in, axis_out, times, table, joined):
         got = [value] + [partner(value, axis_in, step) for step in steps]
-        sent = [partner(times(got[step]).astype(jnp.bfloat16), axis_out, table[step]) for step in steps]
+        if joined:
+            values = [times(got[1])] + together(times, got[2:])
+        else:
+            values = [times(got[step]) for step in steps]
+        sent = [partner(values[step - 1].astype(jnp.bfloat16), axis_out, table[step]) for step in steps]
         own = lax.optimization_barrier(times(value))
         return got, total([own] + sent)
 
@@ -110,15 +117,15 @@
     sent = [partner(values[step].astype(jnp.bfloat16), "col", step) for step in steps]
     first = total([values[0]] + sent).astype(jnp.bfloat16)
 
-    _, second = product(first, "col", "row", by_rows, MIXED)
+    _, second = product(first, "col", "row", by_rows, MIXED, True)
     second = (2.0 * second - panel[0].astype(jnp.float32)).astype(jnp.bfloat16)
-    seconds, third = product(second, "row", "col", by_columns, unmixed)
+    seconds, third = product(second, "row", "col", by_columns, unmixed, False)
     third = (2.0 * third - first.astype(jnp.float32)).astype(jnp.bfloat16)
 
     gathered = [third] + [partner(third, "col", step) for step in steps]
     result = 0.0
-    for step in range(SIDE):
-        value = by_rows(gathered[step])
+    values = [by_rows(gathered[0]), by_rows(gathered[1])] + together(by_rows, gathered[2:])
+    for step, value in enumerate(values):
         back = crossed(value.astype(jnp.bfloat16), step)
         result += jnp.where(col == step, value, back.astype(jnp.float32))
     result = (2.0 * result - picked(seconds, mixed_col).astype(jnp.float32)).astype(jnp.bfloat16)

time: 69.9 us -> 71.6 us (1.024)
  waiting for transfers between devices: 24.2 us -> 27.5 us
  matrix products: 6.02 us -> 5.1 us
  starting transfers between devices: 33.6 us -> 32.8 us
    ppermute x21, waiting for transfers between devices: 19.2 us -> 23 us  [partner(): return lax.ppermute(value, axis, [(i, i ^ step) for i in range(SIDE)])]
    dot_general x8 -> x6, matrix products: 3.72 us -> 2.8 us  [by_rows(): return jnp.dot(panel, whole, preferred_element_type=jnp.float32)]
  transfers between devices with their start and end apart: 27 -> 27, of which waited for: 15 -> 19; matrix products, arithmetic and copies ran while one was open for 9% -> 8% of each run, Pallas kernels for 2% -> 2%
where the time goes in v2:
time: 71.6 us; the launch traced here: 71.4 us
  starting transfers between devices  32.8 us (46%)
  waiting for transfers between devices  27.5 us (38%)
  matrix products  5.1 us (7%)
  local copies, waits for them, and re-layouts  2.44 us (3%)
  between operations  1.48 us (2%)
  Pallas kernels  1.12 us (2%)
  other arithmetic  0.95 us (1%)
    ppermute x21, starting transfers between devices, partner(): return lax.ppermute(value, axis, [(i, i ^ step) for i in range(SIDE)])  28.7 us
    ppermute x21, waiting for transfers between devices, partner(): return lax.ppermute(value, axis, [(i, i ^ step) for i in range(SIDE)])  23 us
    ppermute x4, starting transfers between devices, crossed(): return lax.ppermute(value, ('row', 'col', 'layer'), pairs)  3.59 us
    ppermute x4, waiting for transfers between devices, crossed(): return lax.ppermute(value, ('row', 'col', 'layer'), pairs)  2.93 us
    dot_general x6, matrix products, by_rows(): return jnp.dot(panel, whole, preferred_element_type=jnp.float32)  2.8 us
    dot_general x5, matrix products, by_columns(): return jnp.dot(panel, turned, preferred_element_type=jnp.float32)  2.3 us
    unnamed x2, local copies, waits for them, and re-layouts  1.59 us
  transfers between devices with their start and end apart: 27, of which 19 were waited for; matrix products, arithmetic and copies ran while one was open for 8% of the time, Pallas kernels for 2%

profile of v2, /device:TPU:0, one launch (start us, length us, event | category | flops | bytes accessed | tf_op | source)
XLA Modules:
  0.0 71.4 jit_solution(10430722098552347688)
XLA Ops:
  0.5 0.8 %constant_dynamic-slice_fusion.3 = bf16[32,512]{1,0:T(8,128)(2,1)S(1)} fusion(bf16[64,512]{1,0:T(8,128)(2,1)} %param.5, s32[]{:T(128)S(6)} %select_n.80), kind=kLoop, calls=%fused_computation.48 | loop fusion | bytes 65540 | tf_op jit(solution)/shard_map/dynamic_slice | solution.py:106
  1.6 3.8 %collective-permute-start.3 = (bf16[32,1024]{1,0:T(8,128)(2,1)S(1)}, bf16[32,1024]{1,0:T(8,128)(2,1)S(1)}, u32[]{:S(2)}, u32[]{:S(2)}) collective-permute-start(bf16[32,1024]{1,0:T(8,128)(2,1)S(1)} %maximum_select_fusion), channel_id=1, source_target_pairs={{0,24},{8,16},{16,8},{24,0},{1,25},{9,17},{17,9},{25,1},{2,26},{10... | collective-permute-start | bytes 196616 | tf_op jit(solution)/shard_map/ppermute | solution.py:82
  7.4 1.6 %copy-done = bf16[1024,1024]{1,0:T(8,128)(2,1)S(1)} copy-done((bf16[1024,1024]{1,0:T(8,128)(2,1)S(1)}, bf16[1024,1024]{1,0:T(8,128)(2,1)}, u32[]{:S(2)}) %copy-start) | copy-done | bytes 2097176
  9.0 1.1 %shift.1 = (bf16[1024,1024]{1,0:T(8,128)(2,1)S(1)}, bf16[1024,1024]{1,0:T(8,128)(2,1)S(1)}) custom-call(bf16[1024,1024]{1,0:T(8,128)(2,1)S(1)} %copy-done, f32[1,1]{1,0:T(1,128)} %bitcast.42.low_ref, f32[1,1]{1,0:T(1,128)} %bitcast.43.high_ref), custom_call_target="tpu_custom_call" | custom-call | flops 4194304 | bytes 6291456 | tf_op jit(solution)/shard_map/shift/pallas_call | solution.py:49
  10.8 4.0 %collective-permute-start.6 = (bf16[32,1024]{1,0:T(8,128)(2,1)S(1)}, bf16[32,1024]{1,0:T(8,128)(2,1)S(1)}, u32[]{:S(2)}, u32[]{:S(2)}) collective-permute-start(bf16[32,1024]{1,0:T(8,128)(2,1)S(1)} %get-tuple-element.20), channel_id=1, source_target_pairs={{0,6},{2,4},{4,2},{6,0},{1,7},{3,5},{5,3},{7,1},{8,14},{10,12},{12... | collective-permute-start | bytes 196616 | tf_op jit(solution)/shard_map/ppermute | solution.py:82
  14.8 0.6 collective-permute-start.4
  15.4 2.4 %collective-permute-done.6 = bf16[32,1024]{1,0:T(8,128)(2,1)S(1)} collective-permute-done((bf16[32,1024]{1,0:T(8,128)(2,1)S(1)}, bf16[32,1024]{1,0:T(8,128)(2,1)S(1)}, u32[]{:S(2)}, u32[]{:S(2)}) %collective-permute-start.6) | collective-permute-done | bytes 65568 | tf_op jit(solution)/shard_map/ppermute | solution.py:82
  17.8 2.2 %collective-permute-done.5 = bf16[32,1024]{1,0:T(8,128)(2,1)S(1)} collective-permute-done((bf16[32,1024]{1,0:T(8,128)(2,1)S(1)}, bf16[32,1024]{1,0:T(8,128)(2,1)S(1)}, u32[]{:S(2)}, u32[]{:S(2)}) %collective-permute-start.5) | collective-permute-done | bytes 65568 | tf_op jit(solution)/shard_map/ppermute | solution.py:82
  20.1 2.6 %collective-permute-start.10 = (bf16[32,1024]{1,0:T(8,128)(2,1)S(1)}, bf16[32,1024]{1,0:T(8,128)(2,1)S(1)}, u32[]{:S(2)}, u32[]{:S(2)}) collective-permute-start(bf16[32,1024]{1,0:T(8,128)(2,1)S(1)} %fusion.10), channel_id=1, source_target_pairs={{0,6},{2,4},{4,2},{6,0},{1,7},{3,5},{5,3},{7,1},{8,14},{10,12},{12... | collective-permute-start | bytes 196616 | tf_op jit(solution)/shard_map/ppermute | solution.py:82
  22.7 1.9 %collective-permute-start.7 = (bf16[32,1024]{1,0:T(8,128)(2,1)S(1)}, bf16[32,1024]{1,0:T(8,128)(2,1)S(1)}, u32[]{:S(2)}, u32[]{:S(2)}) collective-permute-start(bf16[32,1024]{1,0:T(8,128)(2,1)S(1)} %fusion.10), channel_id=1, source_target_pairs={{0,2},{2,0},{4,6},{6,4},{1,3},{3,1},{5,7},{7,5},{8,10},{10,8},{12,... | collective-permute-start | bytes 196616 | tf_op jit(solution)/shard_map/ppermute | solution.py:82
  24.6 1.9 %collective-permute-done.10 = bf16[32,1024]{1,0:T(8,128)(2,1)S(1)} collective-permute-done((bf16[32,1024]{1,0:T(8,128)(2,1)S(1)}, bf16[32,1024]{1,0:T(8,128)(2,1)S(1)}, u32[]{:S(2)}, u32[]{:S(2)}) %collective-permute-start.10) | collective-permute-done | bytes 65568 | tf_op jit(solution)/shard_map/ppermute | solution.py:82
  26.5 1.6 %collective-permute-done.9 = bf16[32,1024]{1,0:T(8,128)(2,1)S(1)} collective-permute-done((bf16[32,1024]{1,0:T(8,128)(2,1)S(1)}, bf16[32,1024]{1,0:T(8,128)(2,1)S(1)}, u32[]{:S(2)}, u32[]{:S(2)}) %collective-permute-start.9) | collective-permute-done | bytes 65568 | tf_op jit(solution)/shard_map/ppermute | solution.py:82
  28.6 1.6 %collective-permute-start.12 = (bf16[32,1024]{1,0:T(8,128)(2,1)S(1)}, bf16[32,1024]{1,0:T(8,128)(2,1)S(1)}, u32[]{:S(2)}, u32[]{:S(2)}) collective-permute-start(bf16[32,1024]{1,0:T(8,128)(2,1)S(1)} %get-tuple-element.27), channel_id=1, source_target_pairs={{0,16},{8,24},{16,0},{24,8},{1,17},{9,25},{17,1},{25,9},{2,18},{10... | collective-permute-start | bytes 196616 | tf_op jit(solution)/shard_map/ppermute | solution.py:82
  30.2 1.5 %collective-permute-start.11 = (bf16[32,1024]{1,0:T(8,128)(2,1)S(1)}, bf16[32,1024]{1,0:T(8,128)(2,1)S(1)}, u32[]{:S(2)}, u32[]{:S(2)}) collective-permute-start(bf16[32,1024]{1,0:T(8,128)(2,1)S(1)} %get-tuple-element.26), channel_id=1, source_target_pairs={{0,8},{8,0},{16,24},{24,16},{1,9},{9,1},{17,25},{25,17},{2,10},{10... | collective-permute-start | bytes 196616 | tf_op jit(solution)/shard_map/ppermute | solution.py:82
  33.6 0.8 %collective-permute-done.11 = bf16[32,1024]{1,0:T(8,128)(2,1)S(1)} collective-permute-done((bf16[32,1024]{1,0:T(8,128)(2,1)S(1)}, bf16[32,1024]{1,0:T(8,128)(2,1)S(1)}, u32[]{:S(2)}, u32[]{:S(2)}) %collective-permute-start.11) | collective-permute-done | bytes 65568 | tf_op jit(solution)/shard_map/ppermute | solution.py:82
  34.4 3.6 %collective-permute-done.8 = bf16[32,1024]{1,0:T(8,128)(2,1)S(1)} collective-permute-done((bf16[32,1024]{1,0:T(8,128)(2,1)S(1)}, bf16[32,1024]{1,0:T(8,128)(2,1)S(1)}, u32[]{:S(2)}, u32[]{:S(2)}) %collective-permute-start.8) | collective-permute-done | bytes 65568 | tf_op jit(solution)/shard_map/ppermute | solution.py:82
  38.5 1.6 %collective-permute-start.15 = (bf16[32,1024]{1,0:T(8,128)(2,1)S(1)}, bf16[32,1024]{1,0:T(8,128)(2,1)S(1)}, u32[]{:S(2)}, u32[]{:S(2)}) collective-permute-start(bf16[32,1024]{1,0:T(8,128)(2,1)S(1)} %subtract_convert_fusion.1), channel_id=1, source_target_pairs={{0,16},{8,24},{16,0},{24,8},{1,17},{9,25},{17,1},{25,9},{2,18},{10... | collective-permute-start | bytes 196616 | tf_op jit(solution)/shard_map/ppermute | solution.py:82
  40.1 1.5 %collective-permute-start.13 = (bf16[32,1024]{1,0:T(8,128)(2,1)S(1)}, bf16[32,1024]{1,0:T(8,128)(2,1)S(1)}, u32[]{:S(2)}, u32[]{:S(2)}) collective-permute-start(bf16[32,1024]{1,0:T(8,128)(2,1)S(1)} %subtract_convert_fusion.1), channel_id=1, source_target_pairs={{0,8},{8,0},{16,24},{24,16},{1,9},{9,1},{17,25},{25,17},{2,10},{10... | collective-permute-start | bytes 196616 | tf_op jit(solution)/shard_map/ppermute | solution.py:82
  41.6 1.8 %collective-permute-done.17 = bf16[32,1024]{1,0:T(8,128)(2,1)S(1)} collective-permute-done((bf16[32,1024]{1,0:T(8,128)(2,1)S(1)}, bf16[32,1024]{1,0:T(8,128)(2,1)S(1)}, u32[]{:S(2)}, u32[]{:S(2)}) %collective-permute-start.17) | collective-permute-done | bytes 65568 | tf_op jit(solution)/shard_map/ppermute | solution.py:82
  44.4 2.1 %collective-permute-start.16 = (bf16[32,1024]{1,0:T(8,128)(2,1)S(1)}, bf16[32,1024]{1,0:T(8,128)(2,1)S(1)}, u32[]{:S(2)}, u32[]{:S(2)}) collective-permute-start(bf16[32,1024]{1,0:T(8,128)(2,1)S(1)} %convolution_convert_fusion.2), channel_id=1, source_target_pairs={{0,6},{2,4},{4,2},{6,0},{1,7},{3,5},{5,3},{7,1},{8,14},{10,12},{12... | collective-permute-start | bytes 196616 | tf_op jit(solution)/shard_map/ppermute | solution.py:82
  46.9 1.4 %collective-permute-start.14 = (bf16[32,1024]{1,0:T(8,128)(2,1)S(1)}, bf16[32,1024]{1,0:T(8,128)(2,1)S(1)}, u32[]{:S(2)}, u32[]{:S(2)}) collective-permute-start(bf16[32,1024]{1,0:T(8,128)(2,1)S(1)} %convolution_convert_fusion.3), channel_id=1, source_target_pairs={{0,4},{2,6},{4,0},{6,2},{1,5},{3,7},{5,1},{7,3},{8,12},{10,14},{12... | collective-permute-start | bytes 196616 | tf_op jit(solution)/shard_map/ppermute | solution.py:82
  48.8 2.3 %collective-permute-done.16 = bf16[32,1024]{1,0:T(8,128)(2,1)S(1)} collective-permute-done((bf16[32,1024]{1,0:T(8,128)(2,1)S(1)}, bf16[32,1024]{1,0:T(8,128)(2,1)S(1)}, u32[]{:S(2)}, u32[]{:S(2)}) %collective-permute-start.16) | collective-permute-done | bytes 65568 | tf_op jit(solution)/shard_map/ppermute | solution.py:82
  51.1 3.2 %collective-permute-done.14 = bf16[32,1024]{1,0:T(8,128)(2,1)S(1)} collective-permute-done((bf16[32,1024]{1,0:T(8,128)(2,1)S(1)}, bf16[32,1024]{1,0:T(8,128)(2,1)S(1)}, u32[]{:S(2)}, u32[]{:S(2)}) %collective-permute-start.14) | collective-permute-done | bytes 65568 | tf_op jit(solution)/shard_map/ppermute | solution.py:82
  54.3 2.2 %collective-permute-start.23 = (bf16[32,1024]{1,0:T(8,128)(2,1)S(1)}, bf16[32,1024]{1,0:T(8,128)(2,1)S(1)}, u32[]{:S(2)}, u32[]{:S(2)}) collective-permute-start(bf16[32,1024]{1,0:T(8,128)(2,1)S(1)} %subtract_convert_fusion), channel_id=1, source_target_pairs={{0,6},{2,4},{4,2},{6,0},{1,7},{3,5},{5,3},{7,1},{8,14},{10,12},{12... | collective-permute-start | bytes 196616 | tf_op jit(solution)/shard_map/ppermute | solution.py:82
  56.5 2.3 %collective-permute-start.20 = (bf16[32,1024]{1,0:T(8,128)(2,1)S(1)}, bf16[32,1024]{1,0:T(8,128)(2,1)S(1)}, u32[]{:S(2)}, u32[]{:S(2)}) collective-permute-start(bf16[32,1024]{1,0:T(8,128)(2,1)S(1)} %subtract_convert_fusion), channel_id=1, source_target_pairs={{0,2},{2,0},{4,6},{6,4},{1,3},{3,1},{5,7},{7,5},{8,10},{10,8},{12,... | collective-permute-start | bytes 196616 | tf_op jit(solution)/shard_map/ppermute | solution.py:82
  59.3 1.2 %collective-permute-done.23 = bf16[32,1024]{1,0:T(8,128)(2,1)S(1)} collective-permute-done((bf16[32,1024]{1,0:T(8,128)(2,1)S(1)}, bf16[32,1024]{1,0:T(8,128)(2,1)S(1)}, u32[]{:S(2)}, u32[]{:S(2)}) %collective-permute-start.23) | collective-permute-done | bytes 65568 | tf_op jit(solution)/shard_map/ppermute | solution.py:82
  60.5 1.4 %collective-permute-done.22 = bf16[32,1024]{1,0:T(8,128)(2,1)S(1)} collective-permute-done((bf16[32,1024]{1,0:T(8,128)(2,1)S(1)}, bf16[32,1024]{1,0:T(8,128)(2,1)S(1)}, u32[]{:S(2)}, u32[]{:S(2)}) %collective-permute-start.22) | collective-permute-done | bytes 65568 | tf_op jit(solution)/shard_map/ppermute | solution.py:82
  62.8 0.9 %collective-permute-start.24 = (bf16[32,1024]{1,0:T(8,128)(2,1)S(1)}, bf16[32,1024]{1,0:T(8,128)(2,1)S(1)}, u32[]{:S(2)}, u32[]{:S(2)}) collective-permute-start(bf16[32,1024]{1,0:T(8,128)(2,1)S(1)} %get-tuple-element.17), channel_id=1, source_target_pairs={{0,8},{1,9},{2,18},{3,19},{4,5},{5,4},{6,30},{7,31},{8,0},{9,1},{1... | collective-permute-start | bytes 196616 | tf_op jit(solution)/shard_map/ppermute | solution.py:91
  64.2 2.2 %collective-permute-start.21 = (bf16[32,1024]{1,0:T(8,128)(2,1)S(1)}, bf16[32,1024]{1,0:T(8,128)(2,1)S(1)}, u32[]{:S(2)}, u32[]{:S(2)}) collective-permute-start(bf16[32,1024]{1,0:T(8,128)(2,1)S(1)} %get-tuple-element.32), channel_id=1, source_target_pairs={{0,24},{1,25},{2,3},{3,2},{4,20},{5,21},{6,14},{7,15},{8,16},{9,17... | collective-permute-start | bytes 196616 | tf_op jit(solution)/shard_map/ppermute | solution.py:91
  67.1 2.3 %collective-permute-done.21 = bf16[32,1024]{1,0:T(8,128)(2,1)S(1)} collective-permute-done((bf16[32,1024]{1,0:T(8,128)(2,1)S(1)}, bf16[32,1024]{1,0:T(8,128)(2,1)S(1)}, u32[]{:S(2)}, u32[]{:S(2)}) %collective-permute-start.21) | collective-permute-done | bytes 65568 | tf_op jit(solution)/shard_map/ppermute | solution.py:91
  69.6 1.2 %collective-permute-done.26 = bf16[32,512]{1,0:T(8,128)(2,1)S(1)} collective-permute-done((bf16[32,512]{1,0:T(8,128)(2,1)S(1)}, bf16[32,512]{1,0:T(8,128)(2,1)S(1)}, u32[]{:S(2)}, u32[]{:S(2)}) %collective-permute-start.26) | collective-permute-done | bytes 32800 | tf_op jit(solution)/shard_map/ppermute | solution.py:135
  70.8 0.6 maximum_select_fusion.1
  (50 shorter events, 9.8 us)
Async XLA Ops:
  0.0 1.6 %collective-permute-start = (bf16[64,512]{1,0:T(8,128)(2,1)}, bf16[64,512]{1,0:T(8,128)(2,1)S(1)}, u32[]{:S(2)}, u32[]{:S(2)}) collective-permute-start(bf16[64,512]{1,0:T(8,128)(2,1)} %param.5), channel_id=1, source_target_pairs={{0,1},{1,0},{2,3},{3,2},{4,5},{5,4},{6,7},{7,6},{8,9},{9,8},{10,11... | collective-permute-start | bytes 196616 | tf_op jit(solution)/shard_map/ppermute | solution.py:107
  1.6 8.5 %collective-permute-start.3 = (bf16[32,1024]{1,0:T(8,128)(2,1)S(1)}, bf16[32,1024]{1,0:T(8,128)(2,1)S(1)}, u32[]{:S(2)}, u32[]{:S(2)}) collective-permute-start(bf16[32,1024]{1,0:T(8,128)(2,1)S(1)} %maximum_select_fusion), channel_id=1, source_target_pairs={{0,24},{8,16},{16,8},{24,0},{1,25},{9,17},{17,9},{25,1},{2,26},{10... | collective-permute-start | bytes 196616 | tf_op jit(solution)/shard_map/ppermute | solution.py:82
  5.5 4.7 %collective-permute-start.2 = (bf16[32,1024]{1,0:T(8,128)(2,1)S(1)}, bf16[32,1024]{1,0:T(8,128)(2,1)S(1)}, u32[]{:S(2)}, u32[]{:S(2)}) collective-permute-start(bf16[32,1024]{1,0:T(8,128)(2,1)S(1)} %maximum_select_fusion), channel_id=1, source_target_pairs={{0,16},{8,24},{16,0},{24,8},{1,17},{9,25},{17,1},{25,9},{2,18},{10... | collective-permute-start | bytes 196616 | tf_op jit(solution)/shard_map/ppermute | solution.py:82
  6.0 4.3 %collective-permute-start.1 = (bf16[32,1024]{1,0:T(8,128)(2,1)S(1)}, bf16[32,1024]{1,0:T(8,128)(2,1)S(1)}, u32[]{:S(2)}, u32[]{:S(2)}) collective-permute-start(bf16[32,1024]{1,0:T(8,128)(2,1)S(1)} %maximum_select_fusion), channel_id=1, source_target_pairs={{0,8},{8,0},{16,24},{24,16},{1,9},{9,1},{17,25},{25,17},{2,10},{10... | collective-permute-start | bytes 196616 | tf_op jit(solution)/shard_map/ppermute | solution.py:82
  7.4 1.6 %copy-start = (bf16[1024,1024]{1,0:T(8,128)(2,1)S(1)}, bf16[1024,1024]{1,0:T(8,128)(2,1)}, u32[]{:S(2)}) copy-start(bf16[1024,1024]{1,0:T(8,128)(2,1)} %block_ref) | copy-start | bytes 6291460
  10.8 7.0 %collective-permute-start.6 = (bf16[32,1024]{1,0:T(8,128)(2,1)S(1)}, bf16[32,1024]{1,0:T(8,128)(2,1)S(1)}, u32[]{:S(2)}, u32[]{:S(2)}) collective-permute-start(bf16[32,1024]{1,0:T(8,128)(2,1)S(1)} %get-tuple-element.20), channel_id=1, source_target_pairs={{0,6},{2,4},{4,2},{6,0},{1,7},{3,5},{5,3},{7,1},{8,14},{10,12},{12... | collective-permute-start | bytes 196616 | tf_op jit(solution)/shard_map/ppermute | solution.py:82
  14.8 5.2 %collective-permute-start.5 = (bf16[32,1024]{1,0:T(8,128)(2,1)S(1)}, bf16[32,1024]{1,0:T(8,128)(2,1)S(1)}, u32[]{:S(2)}, u32[]{:S(2)}) collective-permute-start(bf16[32,1024]{1,0:T(8,128)(2,1)S(1)} %get-tuple-element.21), channel_id=1, source_target_pairs={{0,4},{2,6},{4,0},{6,2},{1,5},{3,7},{5,1},{7,3},{8,12},{10,14},{12... | collective-permute-start | bytes 196616 | tf_op jit(solution)/shard_map/ppermute | solution.py:82
  14.8 5.3 %collective-permute-start.4 = (bf16[32,1024]{1,0:T(8,128)(2,1)S(1)}, bf16[32,1024]{1,0:T(8,128)(2,1)S(1)}, u32[]{:S(2)}, u32[]{:S(2)}) collective-permute-start(bf16[32,1024]{1,0:T(8,128)(2,1)S(1)} %get-tuple-element.19), channel_id=1, source_target_pairs={{0,2},{2,0},{4,6},{6,4},{1,3},{3,1},{5,7},{7,5},{8,10},{10,8},{12,... | collective-permute-start | bytes 196616 | tf_op jit(solution)/shard_map/ppermute | solution.py:82
  20.1 6.3 %collective-permute-start.10 = (bf16[32,1024]{1,0:T(8,128)(2,1)S(1)}, bf16[32,1024]{1,0:T(8,128)(2,1)S(1)}, u32[]{:S(2)}, u32[]{:S(2)}) collective-permute-start(bf16[32,1024]{1,0:T(8,128)(2,1)S(1)} %fusion.10), channel_id=1, source_target_pairs={{0,6},{2,4},{4,2},{6,0},{1,7},{3,5},{5,3},{7,1},{8,14},{10,12},{12... | collective-permute-start | bytes 196616 | tf_op jit(solution)/shard_map/ppermute | solution.py:82
  22.7 5.4 %collective-permute-start.9 = (bf16[32,1024]{1,0:T(8,128)(2,1)S(1)}, bf16[32,1024]{1,0:T(8,128)(2,1)S(1)}, u32[]{:S(2)}, u32[]{:S(2)}) collective-permute-start(bf16[32,1024]{1,0:T(8,128)(2,1)S(1)} %fusion.10), channel_id=1, source_target_pairs={{0,4},{2,6},{4,0},{6,2},{1,5},{3,7},{5,1},{7,3},{8,12},{10,14},{12... | collective-permute-start | bytes 196616 | tf_op jit(solution)/shard_map/ppermute | solution.py:82
  22.7 8.9 %collective-permute-start.7 = (bf16[32,1024]{1,0:T(8,128)(2,1)S(1)}, bf16[32,1024]{1,0:T(8,128)(2,1)S(1)}, u32[]{:S(2)}, u32[]{:S(2)}) collective-permute-start(bf16[32,1024]{1,0:T(8,128)(2,1)S(1)} %fusion.10), channel_id=1, source_target_pairs={{0,2},{2,0},{4,6},{6,4},{1,3},{3,1},{5,7},{7,5},{8,10},{10,8},{12,... | collective-permute-start | bytes 196616 | tf_op jit(solution)/shard_map/ppermute | solution.py:82
  28.6 5.0 %collective-permute-start.12 = (bf16[32,1024]{1,0:T(8,128)(2,1)S(1)}, bf16[32,1024]{1,0:T(8,128)(2,1)S(1)}, u32[]{:S(2)}, u32[]{:S(2)}) collective-permute-start(bf16[32,1024]{1,0:T(8,128)(2,1)S(1)} %get-tuple-element.27), channel_id=1, source_target_pairs={{0,16},{8,24},{16,0},{24,8},{1,17},{9,25},{17,1},{25,9},{2,18},{10... | collective-permute-start | bytes 196616 | tf_op jit(solution)/shard_map/ppermute | solution.py:82
  30.2 4.3 %collective-permute-start.11 = (bf16[32,1024]{1,0:T(8,128)(2,1)S(1)}, bf16[32,1024]{1,0:T(8,128)(2,1)S(1)}, u32[]{:S(2)}, u32[]{:S(2)}) collective-permute-start(bf16[32,1024]{1,0:T(8,128)(2,1)S(1)} %get-tuple-element.26), channel_id=1, source_target_pairs={{0,8},{8,0},{16,24},{24,16},{1,9},{9,1},{17,25},{25,17},{2,10},{10... | collective-permute-start | bytes 196616 | tf_op jit(solution)/shard_map/ppermute | solution.py:82
  32.1 5.9 %collective-permute-start.8 = (bf16[32,1024]{1,0:T(8,128)(2,1)S(1)}, bf16[32,1024]{1,0:T(8,128)(2,1)S(1)}, u32[]{:S(2)}, u32[]{:S(2)}) collective-permute-start(bf16[32,1024]{1,0:T(8,128)(2,1)S(1)} %convolution_convert_fusion.4), channel_id=1, source_target_pairs={{0,24},{8,16},{16,8},{24,0},{1,25},{9,17},{17,9},{25,1},{2,26},{10... | collective-permute-start | bytes 196616 | tf_op jit(solution)/shard_map/ppermute | solution.py:82
  38.1 5.3 %collective-permute-start.17 = (bf16[32,1024]{1,0:T(8,128)(2,1)S(1)}, bf16[32,1024]{1,0:T(8,128)(2,1)S(1)}, u32[]{:S(2)}, u32[]{:S(2)}) collective-permute-start(bf16[32,1024]{1,0:T(8,128)(2,1)S(1)} %subtract_convert_fusion.1), channel_id=1, source_target_pairs={{0,24},{8,16},{16,8},{24,0},{1,25},{9,17},{17,9},{25,1},{2,26},{10... | collective-permute-start | bytes 196616 | tf_op jit(solution)/shard_map/ppermute | solution.py:82
  38.5 5.4 %collective-permute-start.15 = (bf16[32,1024]{1,0:T(8,128)(2,1)S(1)}, bf16[32,1024]{1,0:T(8,128)(2,1)S(1)}, u32[]{:S(2)}, u32[]{:S(2)}) collective-permute-start(bf16[32,1024]{1,0:T(8,128)(2,1)S(1)} %subtract_convert_fusion.1), channel_id=1, source_target_pairs={{0,16},{8,24},{16,0},{24,8},{1,17},{9,25},{17,1},{25,9},{2,18},{10... | collective-permute-start | bytes 196616 | tf_op jit(solution)/shard_map/ppermute | solution.py:82
  40.1 6.4 %collective-permute-start.13 = (bf16[32,1024]{1,0:T(8,128)(2,1)S(1)}, bf16[32,1024]{1,0:T(8,128)(2,1)S(1)}, u32[]{:S(2)}, u32[]{:S(2)}) collective-permute-start(bf16[32,1024]{1,0:T(8,128)(2,1)S(1)} %subtract_convert_fusion.1), channel_id=1, source_target_pairs={{0,8},{8,0},{16,24},{24,16},{1,9},{9,1},{17,25},{25,17},{2,10},{10... | collective-permute-start | bytes 196616 | tf_op jit(solution)/shard_map/ppermute | solution.py:82
  43.8 4.9 %collective-permute-start.18 = (bf16[32,1024]{1,0:T(8,128)(2,1)S(1)}, bf16[32,1024]{1,0:T(8,128)(2,1)S(1)}, u32[]{:S(2)}, u32[]{:S(2)}) collective-permute-start(bf16[32,1024]{1,0:T(8,128)(2,1)S(1)} %convolution_convert_fusion.1), channel_id=1, source_target_pairs={{0,2},{2,0},{4,6},{6,4},{1,3},{3,1},{5,7},{7,5},{8,10},{10,8},{12,... | collective-permute-start | bytes 196616 | tf_op jit(solution)/shard_map/ppermute | solution.py:82
  44.4 6.8 %collective-permute-start.16 = (bf16[32,1024]{1,0:T(8,128)(2,1)S(1)}, bf16[32,1024]{1,0:T(8,128)(2,1)S(1)}, u32[]{:S(2)}, u32[]{:S(2)}) collective-permute-start(bf16[32,1024]{1,0:T(8,128)(2,1)S(1)} %convolution_convert_fusion.2), channel_id=1, source_target_pairs={{0,6},{2,4},{4,2},{6,0},{1,7},{3,5},{5,3},{7,1},{8,14},{10,12},{12... | collective-permute-start | bytes 196616 | tf_op jit(solution)/shard_map/ppermute | solution.py:82
  46.9 7.4 %collective-permute-start.14 = (bf16[32,1024]{1,0:T(8,128)(2,1)S(1)}, bf16[32,1024]{1,0:T(8,128)(2,1)S(1)}, u32[]{:S(2)}, u32[]{:S(2)}) collective-permute-start(bf16[32,1024]{1,0:T(8,128)(2,1)S(1)} %convolution_convert_fusion.3), channel_id=1, source_target_pairs={{0,4},{2,6},{4,0},{6,2},{1,5},{3,7},{5,1},{7,3},{8,12},{10,14},{12... | collective-permute-start | bytes 196616 | tf_op jit(solution)/shard_map/ppermute | solution.py:82
  54.3 6.1 %collective-permute-start.23 = (bf16[32,1024]{1,0:T(8,128)(2,1)S(1)}, bf16[32,1024]{1,0:T(8,128)(2,1)S(1)}, u32[]{:S(2)}, u32[]{:S(2)}) collective-permute-start(bf16[32,1024]{1,0:T(8,128)(2,1)S(1)} %subtract_convert_fusion), channel_id=1, source_target_pairs={{0,6},{2,4},{4,2},{6,0},{1,7},{3,5},{5,3},{7,1},{8,14},{10,12},{12... | collective-permute-start | bytes 196616 | tf_op jit(solution)/shard_map/ppermute | solution.py:82
  56.5 5.4 %collective-permute-start.22 = (bf16[32,1024]{1,0:T(8,128)(2,1)S(1)}, bf16[32,1024]{1,0:T(8,128)(2,1)S(1)}, u32[]{:S(2)}, u32[]{:S(2)}) collective-permute-start(bf16[32,1024]{1,0:T(8,128)(2,1)S(1)} %subtract_convert_fusion), channel_id=1, source_target_pairs={{0,4},{2,6},{4,0},{6,2},{1,5},{3,7},{5,1},{7,3},{8,12},{10,14},{12... | collective-permute-start | bytes 196616 | tf_op jit(solution)/shard_map/ppermute | solution.py:82
  56.5 7.2 %collective-permute-start.20 = (bf16[32,1024]{1,0:T(8,128)(2,1)S(1)}, bf16[32,1024]{1,0:T(8,128)(2,1)S(1)}, u32[]{:S(2)}, u32[]{:S(2)}) collective-permute-start(bf16[32,1024]{1,0:T(8,128)(2,1)S(1)} %subtract_convert_fusion), channel_id=1, source_target_pairs={{0,2},{2,0},{4,6},{6,4},{1,3},{3,1},{5,7},{7,5},{8,10},{10,8},{12,... | collective-permute-start | bytes 196616 | tf_op jit(solution)/shard_map/ppermute | solution.py:82
  59.3 7.2 %collective-permute-start.19 = (bf16[32,1024]{1,0:T(8,128)(2,1)S(1)}, bf16[32,1024]{1,0:T(8,128)(2,1)S(1)}, u32[]{:S(2)}, u32[]{:S(2)}) collective-permute-start(bf16[32,1024]{1,0:T(8,128)(2,1)S(1)} %get-tuple-element.34), channel_id=1, source_target_pairs={{0,1},{1,0},{2,26},{3,27},{4,12},{5,13},{6,22},{7,23},{8,9},{9,8},... | collective-permute-start | bytes 196616 | tf_op jit(solution)/shard_map/ppermute | solution.py:91
  62.4 4.3 %collective-permute-start.25 = (bf16[32,1024]{1,0:T(8,128)(2,1)S(1)}, bf16[32,1024]{1,0:T(8,128)(2,1)S(1)}, u32[]{:S(2)}, u32[]{:S(2)}) collective-permute-start(bf16[32,1024]{1,0:T(8,128)(2,1)S(1)} %get-tuple-element.18), channel_id=1, source_target_pairs={{0,16},{1,17},{2,10},{3,11},{4,28},{5,29},{6,7},{7,6},{8,24},{9,25... | collective-permute-start | bytes 196616 | tf_op jit(solution)/shard_map/ppermute | solution.py:91
  62.8 4.3 %collective-permute-start.24 = (bf16[32,1024]{1,0:T(8,128)(2,1)S(1)}, bf16[32,1024]{1,0:T(8,128)(2,1)S(1)}, u32[]{:S(2)}, u32[]{:S(2)}) collective-permute-start(bf16[32,1024]{1,0:T(8,128)(2,1)S(1)} %get-tuple-element.17), channel_id=1, source_target_pairs={{0,8},{1,9},{2,18},{3,19},{4,5},{5,4},{6,30},{7,31},{8,0},{9,1},{1... | collective-permute-start | bytes 196616 | tf_op jit(solution)/shard_map/ppermute | solution.py:91
  64.2 5.2 %collective-permute-start.21 = (bf16[32,1024]{1,0:T(8,128)(2,1)S(1)}, bf16[32,1024]{1,0:T(8,128)(2,1)S(1)}, u32[]{:S(2)}, u32[]{:S(2)}) collective-permute-start(bf16[32,1024]{1,0:T(8,128)(2,1)S(1)} %get-tuple-element.32), channel_id=1, source_target_pairs={{0,24},{1,25},{2,3},{3,2},{4,20},{5,21},{6,14},{7,15},{8,16},{9,17... | collective-permute-start | bytes 196616 | tf_op jit(solution)/shard_map/ppermute | solution.py:91
  69.5 1.3 %collective-permute-start.26 = (bf16[32,512]{1,0:T(8,128)(2,1)S(1)}, bf16[32,512]{1,0:T(8,128)(2,1)S(1)}, u32[]{:S(2)}, u32[]{:S(2)}) collective-permute-start(bf16[32,512]{1,0:T(8,128)(2,1)S(1)} %get-tuple-element.29), channel_id=1, source_target_pairs={{0,1},{1,0},{2,3},{3,2},{4,5},{5,4},{6,7},{7,6},{8,9},{9,8},{10,11... | collective-permute-start | bytes 98312 | tf_op jit(solution)/shard_map/ppermute | solution.py:135
